TPU v7x, 32 devices: a whole 2x2x4 slice. The times are simulated.
32 devices in a mesh: genes: 16 (over z, y, core), cols: 2 (over x).
Axes of the slice: x: 2, y: 2, z: 4, core: 2. Of those that a mesh axis runs over, the one named last changes fastest.
Arguments:
- expression: float32 [384, 40960], P(None, ('genes', 'cols')), may hold values from -200 to 200
- resample: int32 [384], replicated, may hold values from 0 to 383
- labels: int32 [40960, 300], P(('genes', 'cols')), may hold values from 0 to 1, as said below
- ref_kim: float32 [40960], P(('genes', 'cols')), may hold values from 0 to 1
Outputs:
- connectivity: float32 [40960, 300], P(('genes', 'cols'))
- preservation: float32 [2, 300], replicated
Inputs may be any that keep to these rules, and one draw needn't show every extreme that they name: `labels`: each row holds exactly one 1; every module has 32 or more genes.
All inputs are finite; a program needn't handle non-finite values.
Results may differ from a plain program's by a relative error of at most 0.0031.
Values may be sent and summed in bfloat16 or wider, within the bound.
A program may use at most 128 MiB of HBM per device.

v0:
```python
import math
import jax
import jax.numpy as jnp
from jax import lax
from jax.sharding import PartitionSpec as P

G = 40960


def standardize(expression, resample):
    boot = jnp.take(expression, resample, axis=0)
    centered = boot - jnp.mean(boot, axis=0, keepdims=True)
    total = jnp.sum(centered * centered, axis=0, keepdims=True)
    return (centered * lax.rsqrt(total + 1e-06)).astype(jnp.bfloat16)


def local_sums(connectivity, labels, ref_kim):
    member = labels.astype(jnp.float32)
    kim = jnp.sum(connectivity * member, axis=1)
    rowsum = jnp.sum(connectivity, axis=1)
    stacked = jnp.stack(
        [kim, kim * kim, ref_kim, ref_kim * ref_kim, kim * ref_kim, rowsum, jnp.ones_like(kim)],
        axis=1,
    )
    return jnp.dot(
        member.T, stacked, precision=lax.Precision.HIGHEST, preferred_element_type=jnp.float32
    )


def preserve(sums, total_genes):
    counts = sums[:, 6]
    mean_x = sums[:, 0] / (counts * counts)
    var_x = jnp.maximum(sums[:, 1] / (counts * counts * counts) - mean_x * mean_x, 0.0001)
    mean_y = sums[:, 2] / counts
    var_y = jnp.maximum(sums[:, 3] / counts - mean_y * mean_y, 0.01)
    cross = sums[:, 4] / (counts * counts) - mean_x * mean_y
    between = (sums[:, 5] - sums[:, 0]) / (counts * (total_genes - counts))
    density = (mean_x - between) * jnp.sqrt(counts / var_x)
    linked = cross * jnp.sqrt(counts / (var_x * var_y))
    return jnp.stack([density, linked], axis=0)


def tile_term(row_block, column_block, column_ids, module_count):
    scores = lax.dot_general(
        row_block, column_block, (((0,), (0,)), ((), ())), preferred_element_type=jnp.float32
    )
    squares = scores * scores
    adjacency = (squares * squares * squares).astype(jnp.bfloat16)
    member_block = (
        column_ids[:, None] == jnp.arange(module_count, dtype=jnp.int32)[None, :]
    ).astype(jnp.bfloat16)
    return jnp.dot(adjacency, member_block, preferred_element_type=jnp.float32)


def add_tiles(carried, row_block, piece, every_ids, shard_width, module_count):
    span_width = piece.shape[1]
    column_step = shard_width * math.gcd(span_width // shard_width, 8)
    steps_total = span_width // column_step

    def one_step(step_index, accumulated):
        columns = lax.dynamic_slice_in_dim(piece, step_index * column_step, column_step, 1)
        column_ids = lax.dynamic_slice_in_dim(every_ids, step_index * column_step, column_step, 0)
        return accumulated + tile_term(row_block, columns, column_ids, module_count)

    return lax.fori_loop(0, steps_total, one_step, carried)


def local(expression, resample, labels, ref_kim):
    scaled = standardize(expression, resample)
    module_count = labels.shape[1]
    shard_width = scaled.shape[1]
    module_ids = jnp.sum(labels * jnp.arange(module_count, dtype=jnp.int32)[None, :], axis=1)
    row_block = lax.all_gather(scaled, "cols", axis=1, tiled=True)
    panel_ids = lax.all_gather(module_ids, "genes", axis=0, tiled=True)
    initial = jnp.zeros((row_block.shape[1], module_count), jnp.float32)
    partial_value = add_tiles(
        initial,
        row_block,
        lax.all_gather(scaled, "genes", axis=1, tiled=True),
        panel_ids,
        shard_width,
        module_count,
    )
    connectivity = lax.psum_scatter(partial_value, "cols", scatter_dimension=0, tiled=True)
    sums = lax.psum(local_sums(connectivity, labels, ref_kim), ("genes", "cols"))
    return (connectivity, preserve(sums, G))


def solution(mesh):
    placed = (P(None, ("genes", "cols")), P(), P(("genes", "cols"), None), P(("genes", "cols")))
    return jax.shard_map(
        local,
        mesh=mesh,
        in_specs=placed,
        out_specs=(P(("genes", "cols"), None), P()),
        check_vma=False,
    )
```

profile of v0, /device:TPU:0, one launch (start us, length us, event | category | flops | bytes accessed | tf_op | source)
XLA Modules:
  0.0 391.7 jit_solution(1327400909456358095)
XLA Ops:
  7.2 0.0 all-gather.6.cloned.1.call-start
  7.2 0.8 compare_select_fusion
  8.0 0.7 compare_and_fusion
  8.8 2.7 gather_fusion
  11.5 1.9 select_reduce_fusion
  13.4 0.2 copy-done.2
  13.6 0.3 multiply_reduce_fusion
  14.0 1.3 multiply_convert_fusion
  15.2 0.0 all-gather.6.cloned.1.call-update
  15.3 0.0 all-gather.4.cloned.1.call-start
  15.3 0.7 all-gather.4.cloned.1.call-update
  16.0 0.0 reduce-scatter.2.cloned.1.call-start
  16.1 0.2 multiply_reduce_fusion.2
  16.3 23.3 %all-gather = s32[16,1,1280]{2,1,0:T(1,128)S(1)} all-gather(s32[1,1,1280]{2,1,0:T(1,128)S(1)} %reshape.229), channel_id=1, replica_groups=mesh['genes'=16,'cols'=2] {'genes'}, dimensions={0}, use_global_device_ids=true | all-gather | bytes 87040 | tf_op jit(solution)/shard_map/all_gather | solution.py:74
  39.6 10.2 %all-gather.6.cloned.1.call-done = bf16[384,2560]{1,0:T(8,128)(2,1)} async-done(((bf16[384,1280]{1,0:T(8,128)(2,1)}), bf16[384,2560]{1,0:T(8,128)(2,1)}) %all-gather.6.cloned.1.call-update) | async-done | bytes 1966096 | tf_op jit(solution)/shard_map/all_gather | solution.py:73
  49.8 122.7 %all-gather.4.cloned.1.call-done = bf16[384,20480]{1,0:T(8,128)(2,1)} async-done(((bf16[384,1280]{1,0:T(8,128)(2,1)}), bf16[384,20480]{1,0:T(8,128)(2,1)}) %all-gather.4.cloned.1.call-update) | async-done | bytes 15728656 | tf_op jit(solution)/shard_map/all_gather | solution.py:79
  172.5 124.2 %while.14 = (s32[]{:T(128)}, f32[2560,300]{0,1:T(8,128)}, bf16[384,20480]{1,0:T(8,128)(2,1)}, bf16[384,2560]{1,0:T(8,128)(2,1)}, s32[20480]{0:T(1024)S(1)}, /*index=5*/s32[]{:T(128)}, s32[]{:T(128)}, s32[]{:T(128)}, s32[]{:T(128)}) while((s32[]{:T(128)}, f32[2560,300]{0,1:T(8,128)}, bf16[384,20480]{1,0:T(8,128)(2,1)}, ...), condition=%wide.region_4.5_spmd.clone, body=%wide.region_3.4_spmd.clone.sunk | while | flops 35970764800 | bytes 120955040 | solution.py:65
  172.5 37.4 %fusion.clone.9 = bf16[2560,10240]{0,1:T(8,128)(2,1)} fusion(bf16[384,2560]{1,0:T(8,128)(2,1)} %get-tuple-element.184, bf16[384,20480]{1,0:T(8,128)(2,1)} %get-tuple-element.183, s32[]{:T(128)S(6)} %select_n.27), kind=kOutput, calls=%fused_computation.2.clone.clone.clone.clone.clone.2.clone.1 | convolution fusion | flops 20237516800 | bytes 62259204 | tf_op jit(solution)/shard_map/while/body/eval_jaxpr/dot_general | solution.py:44
  209.9 24.2 %fusion.47 = f32[2560,300]{0,1:T(8,128)} fusion(s32[10240]{0:T(1024)S(1)} %dynamic_slice.28, f32[2560,300]{0,1:T(8,128)} %get-tuple-element.173, pred[]{:T(512)S(6)} %compare.3, bf16[2560,10240]{0,1:T(8,128)(2,1)} %fusion.clone.9), kind=kOutput, calls=%fused_computation.7.clone.3 | convolution fusion | flops 15733248000 | bytes 58613760 | tf_op jit(solution)/shard_map/while/body/eval_jaxpr/dot_general | solution.py:52
  234.1 37.4 %fusion.clone.9 = bf16[2560,10240]{0,1:T(8,128)(2,1)} fusion(bf16[384,2560]{1,0:T(8,128)(2,1)} %get-tuple-element.184, bf16[384,20480]{1,0:T(8,128)(2,1)} %get-tuple-element.183, s32[]{:T(128)S(6)} %select_n.27), kind=kOutput, calls=%fused_computation.2.clone.clone.clone.clone.clone.2.clone.1 | convolution fusion | flops 20237516800 | bytes 62259204 | tf_op jit(solution)/shard_map/while/body/eval_jaxpr/dot_general | solution.py:44
  271.6 25.1 %fusion.47 = f32[2560,300]{0,1:T(8,128)} fusion(s32[10240]{0:T(1024)S(1)} %dynamic_slice.28, f32[2560,300]{0,1:T(8,128)} %get-tuple-element.173, pred[]{:T(512)S(6)} %compare.3, bf16[2560,10240]{0,1:T(8,128)(2,1)} %fusion.clone.9), kind=kOutput, calls=%fused_computation.7.clone.3 | convolution fusion | flops 15733248000 | bytes 58613760 | tf_op jit(solution)/shard_map/while/body/eval_jaxpr/dot_general | solution.py:52
  296.7 0.0 reduce-scatter.2.cloned.1.call-update
  296.7 0.7 copy-done.5
  297.4 40.6 %reduce-scatter.2.cloned.1.call-done = f32[1280,300]{0,1:T(8,128)} async-done(((f32[2560,300]{0,1:T(8,128)}), f32[1280,300]{0,1:T(8,128)}) %reduce-scatter.2.cloned.1.call-update) | async-done | bytes 1536016 | tf_op jit(solution)/shard_map/reduce_scatter | solution.py:84
  338.0 1.6 fusion.26
  339.7 0.6 stack.27
  340.3 0.6 stack.28
  340.9 0.6 stack_broadcast_in_dim.3
  341.5 1.4 stack.29
  342.9 2.1 fusion.12
  345.0 39.5 %psum.7 = f32[300,7]{0,1:T(8,128)S(1)} all-reduce(f32[300,7]{0,1:T(8,128)S(1)} %fusion.12), channel_id=1, replica_groups=mesh['genes'=16,'cols'=2] {'genes','cols'}, use_global_device_ids=true, to_apply=%region_8.9 | all-reduce | flops 2100 | bytes 16800 | tf_op jit(solution)/shard_map/psum | solution.py:85
  384.6 0.6 pad_maximum_fusion
  (24 shorter events, 0.1 us)
Async XLA Ops:
  7.2 1.6 copy-start
  7.2 42.6 %all-gather.6.cloned.1.call-start = ((), (), s32[]{:S(2)}) async-start(), calls=%async_computation.2 | async-start | bytes 2949120 | tf_op jit(solution)/shard_map/all_gather | solution.py:73
  11.5 2.1 copy-start.2
  14.0 2.1 copy-start.3
  15.3 157.2 %all-gather.4.cloned.1.call-start = ((), (), s32[]{:S(2)}) async-start(), calls=%async_computation.1 | async-start | bytes 16711680 | tf_op jit(solution)/shard_map/all_gather | solution.py:79
  16.0 322.0 %reduce-scatter.2.cloned.1.call-start = ((), (), s32[]{:S(2)}) async-start(), calls=%async_computation.3 | async-start | bytes 4669440 | tf_op jit(solution)/shard_map/reduce_scatter | solution.py:84
  296.7 0.7 copy-start.5
  296.7 41.4 %copy-start.4 = (s32[1280,300]{0,1:T(8,128)S(1)}, s32[1280,300]{0,1:T(8,128)}, u32[]{:S(2)}) copy-start(s32[1280,300]{0,1:T(8,128)} %param.8) | copy-start | bytes 4608004
  297.4 87.8 %copy-start.1 = (f32[384,1280]{1,0:T(8,128)S(1)}, f32[384,1280]{1,0:T(8,128)}, u32[]{:S(2)}) copy-start(f32[384,1280]{1,0:T(8,128)} %param.6) | copy-start | bytes 5898244
Sparse Core Ops, SparseCore 0:
  15.4 34.3 all-gather.5
  52.6 119.7 all-gather.3
  296.8 41.1 reduce-scatter.1
where the time goes:
time: 392 us
  waiting for transfers between devices  174 us (44%)
  matrix products  126 us (32%)
  blocking collectives  62.8 us (16%)
  between operations  13.9 us (4%)
  other arithmetic  7.47 us (2%)
  local copies, waits for them, and re-layouts  6.83 us (2%)
    all_gather x1, waiting for transfers between devices, local(): lax.all_gather(scaled, 'genes', axis=1, tiled=True)  123 us
    dot_general x2, matrix products, tile_term(): lax.dot_general(row_block, column_block, (((0,), (0,)), ((), ())), prefer...  74.9 us
    dot_general x2, matrix products, tile_term(): return jnp.dot(adjacency, member_block, preferred_element_type=jnp.float32)  49.3 us
    reduce_scatter x1, waiting for transfers between devices, local(): lax.psum_scatter(partial_value, 'cols', scatter_dimension=0, tiled=True)  40.6 us
    psum x1, blocking collectives, local(): lax.psum(local_sums(connectivity, labels, ref_kim), ('genes', 'cols'))  39.5 us
    all_gather x1, blocking collectives, local(): panel_ids = lax.all_gather(module_ids, 'genes', axis=0, tiled=True)  23.3 us
    all_gather x1, waiting for transfers between devices, local(): row_block = lax.all_gather(scaled, 'cols', axis=1, tiled=True)  10.2 us
  transfers between devices with their start and end apart: 3, of which 3 were waited for; matrix products, arithmetic and copies ran while one was open for 0% of the time, Pallas kernels for 0%

commit v1 on v0

--- a/solution.py
+++ b/solution.py
@@ -82,7 +82,7 @@
         module_count,
     )
     connectivity = lax.psum_scatter(partial_value, "cols", scatter_dimension=0, tiled=True)
-    sums = lax.psum(local_sums(connectivity, labels, ref_kim), ("genes", "cols"))
+    sums = lax.psum(lax.psum(local_sums(connectivity, labels, ref_kim), "genes"), "cols")
     return (connectivity, preserve(sums, G))
 
 

time: 392 us -> 421 us (1.074)
  blocking collectives: 62.8 us -> 91.5 us
    psum x1 -> x2, blocking collectives: 39.5 us -> 68.2 us  [the longest x1 61.1 us: local(): lax.psum(local_sums(connectivity, labels, ref_kim), 'genes')]
where the time goes in v1:
time: 421 us; the launch traced here: 420 us
  waiting for transfers between devices  174 us (41%)
  matrix products  126 us (30%)
  blocking collectives  91.5 us (22%)
  between operations  13.9 us (3%)
  other arithmetic  7.47 us (2%)
  local copies, waits for them, and re-layouts  6.83 us (2%)
    all_gather x1, waiting for transfers between devices, local(): lax.all_gather(scaled, 'genes', axis=1, tiled=True)  123 us
    dot_general x2, matrix products, tile_term(): lax.dot_general(row_block, column_block, (((0,), (0,)), ((), ())), prefer...  74.9 us
    psum x1, blocking collectives, local(): lax.psum(local_sums(connectivity, labels, ref_kim), 'genes')  61.1 us
    dot_general x2, matrix products, tile_term(): return jnp.dot(adjacency, member_block, preferred_element_type=jnp.float32)  49.3 us
    reduce_scatter x1, waiting for transfers between devices, local(): lax.psum_scatter(partial_value, 'cols', scatter_dimension=0, tiled=True)  40.7 us
    all_gather x1, blocking collectives, local(): panel_ids = lax.all_gather(module_ids, 'genes', axis=0, tiled=True)  23.3 us
    all_gather x1, waiting for transfers between devices, local(): row_block = lax.all_gather(scaled, 'cols', axis=1, tiled=True)  10.2 us
  transfers between devices with their start and end apart: 3, of which 3 were waited for; matrix products, arithmetic and copies ran while one was open for 0% of the time, Pallas kernels for 0%

profile of v1, /device:TPU:0, one launch (start us, length us, event | category | flops | bytes accessed | tf_op | source)
XLA Modules:
  0.0 420.4 jit_solution(6319321116603394755)
XLA Ops:
  7.2 0.0 all-gather.6.cloned.1.call-start
  7.2 0.8 compare_select_fusion
  8.0 0.7 compare_and_fusion
  8.8 2.7 gather_fusion
  11.5 1.9 select_reduce_fusion
  13.4 0.2 copy-done.2
  13.6 0.3 multiply_reduce_fusion
  14.0 1.3 multiply_convert_fusion
  15.2 0.0 all-gather.6.cloned.1.call-update
  15.3 0.0 all-gather.4.cloned.1.call-start
  15.3 0.7 all-gather.4.cloned.1.call-update
  16.0 0.0 reduce-scatter.2.cloned.1.call-start
  16.1 0.2 multiply_reduce_fusion.2
  16.3 23.3 %all-gather = s32[16,1,1280]{2,1,0:T(1,128)S(1)} all-gather(s32[1,1,1280]{2,1,0:T(1,128)S(1)} %reshape.229), channel_id=1, replica_groups=mesh['genes'=16,'cols'=2] {'genes'}, dimensions={0}, use_global_device_ids=true | all-gather | bytes 87040 | tf_op jit(solution)/shard_map/all_gather | solution.py:74
  39.6 10.2 %all-gather.6.cloned.1.call-done = bf16[384,2560]{1,0:T(8,128)(2,1)} async-done(((bf16[384,1280]{1,0:T(8,128)(2,1)}), bf16[384,2560]{1,0:T(8,128)(2,1)}) %all-gather.6.cloned.1.call-update) | async-done | bytes 1966096 | tf_op jit(solution)/shard_map/all_gather | solution.py:73
  49.8 122.7 %all-gather.4.cloned.1.call-done = bf16[384,20480]{1,0:T(8,128)(2,1)} async-done(((bf16[384,1280]{1,0:T(8,128)(2,1)}), bf16[384,20480]{1,0:T(8,128)(2,1)}) %all-gather.4.cloned.1.call-update) | async-done | bytes 15728656 | tf_op jit(solution)/shard_map/all_gather | solution.py:79
  172.5 124.2 %while.14 = (s32[]{:T(128)}, f32[2560,300]{0,1:T(8,128)}, bf16[384,20480]{1,0:T(8,128)(2,1)}, bf16[384,2560]{1,0:T(8,128)(2,1)}, s32[20480]{0:T(1024)S(1)}, /*index=5*/s32[]{:T(128)}, s32[]{:T(128)}, s32[]{:T(128)}, s32[]{:T(128)}) while((s32[]{:T(128)}, f32[2560,300]{0,1:T(8,128)}, bf16[384,20480]{1,0:T(8,128)(2,1)}, ...), condition=%wide.region_4.5_spmd.clone, body=%wide.region_3.4_spmd.clone.sunk | while | flops 35970764800 | bytes 120955040 | solution.py:65
  172.5 37.4 %fusion.clone.9 = bf16[2560,10240]{0,1:T(8,128)(2,1)} fusion(bf16[384,2560]{1,0:T(8,128)(2,1)} %get-tuple-element.184, bf16[384,20480]{1,0:T(8,128)(2,1)} %get-tuple-element.183, s32[]{:T(128)S(6)} %select_n.27), kind=kOutput, calls=%fused_computation.2.clone.clone.clone.clone.clone.2.clone.1 | convolution fusion | flops 20237516800 | bytes 62259204 | tf_op jit(solution)/shard_map/while/body/eval_jaxpr/dot_general | solution.py:44
  209.9 24.2 %fusion.47 = f32[2560,300]{0,1:T(8,128)} fusion(s32[10240]{0:T(1024)S(1)} %dynamic_slice.28, f32[2560,300]{0,1:T(8,128)} %get-tuple-element.173, pred[]{:T(512)S(6)} %compare.3, bf16[2560,10240]{0,1:T(8,128)(2,1)} %fusion.clone.9), kind=kOutput, calls=%fused_computation.7.clone.3 | convolution fusion | flops 15733248000 | bytes 58613760 | tf_op jit(solution)/shard_map/while/body/eval_jaxpr/dot_general | solution.py:52
  234.1 37.4 %fusion.clone.9 = bf16[2560,10240]{0,1:T(8,128)(2,1)} fusion(bf16[384,2560]{1,0:T(8,128)(2,1)} %get-tuple-element.184, bf16[384,20480]{1,0:T(8,128)(2,1)} %get-tuple-element.183, s32[]{:T(128)S(6)} %select_n.27), kind=kOutput, calls=%fused_computation.2.clone.clone.clone.clone.clone.2.clone.1 | convolution fusion | flops 20237516800 | bytes 62259204 | tf_op jit(solution)/shard_map/while/body/eval_jaxpr/dot_general | solution.py:44
  271.6 25.1 %fusion.47 = f32[2560,300]{0,1:T(8,128)} fusion(s32[10240]{0:T(1024)S(1)} %dynamic_slice.28, f32[2560,300]{0,1:T(8,128)} %get-tuple-element.173, pred[]{:T(512)S(6)} %compare.3, bf16[2560,10240]{0,1:T(8,128)(2,1)} %fusion.clone.9), kind=kOutput, calls=%fused_computation.7.clone.3 | convolution fusion | flops 15733248000 | bytes 58613760 | tf_op jit(solution)/shard_map/while/body/eval_jaxpr/dot_general | solution.py:52
  296.7 0.7 copy-done.5
  297.4 40.7 %reduce-scatter.2.cloned.1.call-done = f32[1280,300]{0,1:T(8,128)} async-done(((f32[2560,300]{0,1:T(8,128)}), f32[1280,300]{0,1:T(8,128)}) %reduce-scatter.2.cloned.1.call-update) | async-done | bytes 1536016 | tf_op jit(solution)/shard_map/reduce_scatter | solution.py:84
  338.1 1.6 fusion.26
  339.8 0.6 stack.27
  340.4 0.6 stack.28
  340.9 0.6 stack_broadcast_in_dim.3
  341.5 1.4 stack.29
  342.9 2.1 fusion.12
  345.0 61.1 %psum.14 = f32[300,7]{0,1:T(8,128)S(1)} all-reduce(f32[300,7]{0,1:T(8,128)S(1)} %fusion.12), channel_id=1, replica_groups=mesh['genes'=16,'cols'=2] {'genes'}, use_global_device_ids=true, to_apply=%region_8.9 | all-reduce | flops 2100 | bytes 16800 | tf_op jit(solution)/shard_map/psum | solution.py:85
  406.1 7.1 %psum.15 = f32[300,7]{0,1:T(8,128)S(1)} all-reduce(f32[300,7]{0,1:T(8,128)S(1)} %psum.14), channel_id=1, replica_groups=mesh['genes'=16,'cols'=2] {'cols'}, use_global_device_ids=true, to_apply=%region_9.10 | all-reduce | flops 2100 | bytes 16800 | tf_op jit(solution)/shard_map/psum | solution.py:85
  413.3 0.6 pad_maximum_fusion
  (25 shorter events, 0.2 us)
Async XLA Ops:
  7.2 1.6 copy-start
  7.2 42.6 %all-gather.6.cloned.1.call-start = ((), (), s32[]{:S(2)}) async-start(), calls=%async_computation.2 | async-start | bytes 2949120 | tf_op jit(solution)/shard_map/all_gather | solution.py:73
  11.5 2.1 copy-start.2
  14.0 2.1 copy-start.3
  15.3 157.2 %all-gather.4.cloned.1.call-start = ((), (), s32[]{:S(2)}) async-start(), calls=%async_computation.1 | async-start | bytes 16711680 | tf_op jit(solution)/shard_map/all_gather | solution.py:79
  16.0 322.1 %reduce-scatter.2.cloned.1.call-start = ((), (), s32[]{:S(2)}) async-start(), calls=%async_computation.3 | async-start | bytes 4669440 | tf_op jit(solution)/shard_map/reduce_scatter | solution.py:84
  296.7 0.7 copy-start.5
  296.7 41.4 %copy-start.4 = (s32[1280,300]{0,1:T(8,128)S(1)}, s32[1280,300]{0,1:T(8,128)}, u32[]{:S(2)}) copy-start(s32[1280,300]{0,1:T(8,128)} %param.8) | copy-start | bytes 4608004
  297.4 116.5 %copy-start.1 = (f32[384,1280]{1,0:T(8,128)S(1)}, f32[384,1280]{1,0:T(8,128)}, u32[]{:S(2)}) copy-start(f32[384,1280]{1,0:T(8,128)} %param.6) | copy-start | bytes 5898244
Sparse Core Ops, SparseCore 0:
  15.4 34.3 all-gather.5
  52.6 119.7 all-gather.3
  296.8 41.1 reduce-scatter.1
